TPU v7x, 32 devices: a whole 2x2x4 slice. The times are simulated.
32 devices in a mesh: dp: 8 (over y, x, core), tensor: 4 (over z).
Axes of the slice: x: 2, y: 2, z: 4, core: 2. Of those that a mesh axis runs over, the one named last changes fastest.
Arguments:
- images: bfloat16 [32, 320, 1024], P('dp', None, 'tensor'), may hold values from -6 to 6
- lengths: int32 [32], P('dp'), may hold values from 224 to 320, as said below
- cotangent: bfloat16 [32, 320, 1024], P('dp', None, 'tensor'), may hold values from -6 to 6
- norm1_gain: float32 [1024], replicated, may hold values from 0.5 to 1.5
- norm1_shift: float32 [1024], replicated, may hold values from -1.75 to 1.75
- w_qkv: bfloat16 [1024, 3, 1024], P(None, None, 'tensor'), may hold values from -0.1875 to 0.1875
- qv_bias: float32 [2, 1024], P(None, 'tensor'), may hold values from -3 to 3
- w_proj: bfloat16 [1024, 1024], P('tensor'), may hold values from -1.5 to 1.5
- proj_bias: float32 [1024], replicated, may hold values from -3 to 3
- norm2_gain: float32 [1024], replicated, may hold values from 0.5 to 1.5
- norm2_shift: float32 [1024], replicated, may hold values from -1.75 to 1.75
- w_fc1: bfloat16 [1024, 4096], P(None, 'tensor'), may hold values from -0.1875 to 0.1875
- fc1_bias: float32 [4096], P('tensor'), may hold values from -3 to 3
- w_fc2: bfloat16 [4096, 1024], P('tensor'), may hold values from -0.09375 to 0.09375
- fc2_bias: float32 [1024], replicated, may hold values from -3 to 3
Outputs:
- output: bfloat16 [32, 320, 1024], P('dp', None, 'tensor')
- input_grad: bfloat16 [32, 320, 1024], P('dp', None, 'tensor')
- grad_norm1_gain: float32 [1024], replicated
- grad_norm1_shift: float32 [1024], replicated
- grad_w_qkv: float32 [1024, 3, 1024], P(None, None, 'tensor')
- grad_qv_bias: float32 [2, 1024], P(None, 'tensor')
- grad_w_proj: float32 [1024, 1024], P('tensor')
- grad_proj_bias: float32 [1024], replicated
- grad_norm2_gain: float32 [1024], replicated
- grad_norm2_shift: float32 [1024], replicated
- grad_w_fc1: float32 [1024, 4096], P(None, 'tensor')
- grad_fc1_bias: float32 [4096], P('tensor')
- grad_w_fc2: float32 [4096, 1024], P('tensor')
- grad_fc2_bias: float32 [1024], replicated
Inputs may be any that keep to these rules, and one draw needn't show every extreme that they name: lengths[i] is the number of valid slots of image i, which come first; some image has all 320 slots valid in every draw.
All inputs are finite; a program needn't handle non-finite values.
Results may differ from a plain program's by a relative error of at most 0.02.
Values may be sent and summed in bfloat16 or wider, within the bound.
A program may use at most 192 MiB of HBM per device.

v0:
```python
import jax
import jax.numpy as jnp
from jax import lax
from jax.sharding import PartitionSpec as P

HEAD_DIM = 64
EPS = 1e-06
MASKED = -1e30


def norm_rows(values, gain_row, shift_row):
    row_mean = jnp.mean(values, axis=-1, keepdims=True)
    centered = values - row_mean
    spread = jnp.mean(centered * centered, axis=-1, keepdims=True)
    inverse = lax.rsqrt(spread + EPS)
    unit_rows = centered * inverse
    return (unit_rows * gain_row + shift_row, unit_rows, inverse)


def norm_back(gradient, unit_rows, inverse, gain_row):
    scaled = gradient * gain_row
    first_mean = jnp.mean(scaled, axis=-1, keepdims=True)
    cross_mean = jnp.mean(scaled * unit_rows, axis=-1, keepdims=True)
    return inverse * (scaled - first_mean - unit_rows * cross_mean)


def scores_of(queries, key_heads, key_mask, score_scale):
    raw_scores = (
        jnp.einsum("bqhe,bkhe->bhqk", queries, key_heads, preferred_element_type=jnp.float32)
        * score_scale
    )
    return jnp.where(key_mask, raw_scores, MASKED)


def exact_gelu(values):
    return jax.nn.gelu(values, approximate=False)


def per_device(
    images,
    lengths,
    cotangent,
    norm1_gain,
    norm1_shift,
    w_qkv,
    qv_bias,
    w_proj,
    proj_bias,
    norm2_gain,
    norm2_shift,
    w_fc1,
    fc1_bias,
    w_fc2,
    fc2_bias,
):
    images_here, slot_count, col_count = images.shape
    model_width = w_qkv.shape[0]
    local_width = w_qkv.shape[2]
    heads_here = local_width // HEAD_DIM
    row_count = images_here * slot_count
    score_scale = HEAD_DIM ** (-0.5)
    first_col = lax.axis_index("tensor") * col_count
    full_images, full_cot = (
        lax.all_gather(images, "tensor", axis=2, tiled=True),
        lax.all_gather(cotangent, "tensor", axis=2, tiled=True),
    )
    slot_ids = jnp.arange(slot_count, dtype=jnp.int32)
    valid_slots = (slot_ids[None, :] < lengths[:, None]).astype(jnp.float32)
    keep_rows = valid_slots.reshape(row_count, 1)
    row_values = full_images.reshape(row_count, model_width).astype(jnp.float32) * keep_rows
    normed1, unit1, inverse1 = norm_rows(row_values, norm1_gain, norm1_shift)
    normed1 = normed1.astype(jnp.bfloat16)
    qkv_bias = jnp.concatenate([qv_bias[0], jnp.zeros_like(qv_bias[0]), qv_bias[1]])
    w_flat = w_qkv.reshape(model_width, 3 * local_width)
    qkv_rows = (jnp.dot(normed1, w_flat, preferred_element_type=jnp.float32) + qkv_bias).astype(
        jnp.bfloat16
    )
    qkv_rows = qkv_rows.reshape(images_here, slot_count, 3, heads_here, HEAD_DIM)
    queries = qkv_rows[:, :, 0]
    key_heads = qkv_rows[:, :, 1]
    value_heads = qkv_rows[:, :, 2]
    key_mask = valid_slots[:, None, None, :] > 0
    scores = scores_of(queries, key_heads, key_mask, score_scale)
    row_top = jnp.max(scores, axis=-1, keepdims=True)
    shifted = jnp.exp(scores - row_top)
    row_total = jnp.sum(shifted, axis=-1, keepdims=True)
    probability = (shifted / row_total).astype(jnp.bfloat16)
    log_total = row_top + jnp.log(row_total)
    mixed = jnp.einsum(
        "bhqk,bkhe->bqhe", probability, value_heads, preferred_element_type=jnp.float32
    ).astype(jnp.bfloat16)
    mixed_rows = mixed.reshape(row_count, local_width)
    attn_part = jnp.dot(mixed_rows, w_proj, preferred_element_type=jnp.float32)
    middle = (
        row_values
        + lax.psum(attn_part.astype(jnp.bfloat16), "tensor").astype(jnp.float32)
        + proj_bias
    )
    normed2, unit2, inverse2 = norm_rows(middle, norm2_gain, norm2_shift)
    normed2 = normed2.astype(jnp.bfloat16)
    pre_act = jnp.dot(normed2, w_fc1, preferred_element_type=jnp.float32) + fc1_bias
    activated = exact_gelu(pre_act).astype(jnp.bfloat16)
    ff_part = jnp.dot(activated, w_fc2, preferred_element_type=jnp.float32)
    ff_share = lax.psum_scatter(
        ff_part.astype(jnp.bfloat16), "tensor", scatter_dimension=1, tiled=True
    ).astype(jnp.float32)
    middle_cols = lax.dynamic_slice_in_dim(middle, first_col, col_count, 1)
    bias_cols = lax.dynamic_slice_in_dim(fc2_bias, first_col, col_count, 0)
    output = ((middle_cols + ff_share + bias_cols) * keep_rows).astype(jnp.bfloat16)
    output = output.reshape(images_here, slot_count, col_count)
    grad_out = full_cot.reshape(row_count, model_width).astype(jnp.float32) * keep_rows
    grad_ff = grad_out.astype(jnp.bfloat16)
    grad_fc2_bias = jnp.sum(grad_ff, axis=0, dtype=jnp.float32)
    grad_w_fc2 = jnp.einsum("rf,rd->fd", activated, grad_ff, preferred_element_type=jnp.float32)
    grad_act = jnp.einsum("rd,fd->rf", grad_ff, w_fc2, preferred_element_type=jnp.float32)
    gelu_pull = jax.vjp(exact_gelu, pre_act)[1]
    grad_pre = gelu_pull(grad_act)[0].astype(jnp.bfloat16)
    grad_fc1_bias = jnp.sum(grad_pre, axis=0, dtype=jnp.float32)
    grad_w_fc1 = jnp.einsum("rd,rf->df", normed2, grad_pre, preferred_element_type=jnp.float32)
    hidden_part = jnp.einsum("rf,df->rd", grad_pre, w_fc1, preferred_element_type=jnp.float32)
    grad_normed2 = lax.psum(hidden_part.astype(jnp.bfloat16), "tensor").astype(jnp.float32)
    grad_norm2_gain = jnp.sum(grad_normed2 * unit2, axis=0)
    grad_norm2_shift = jnp.sum(grad_normed2, axis=0)
    grad_middle = grad_out + norm_back(grad_normed2, unit2, inverse2, norm2_gain)
    grad_attn = grad_middle.astype(jnp.bfloat16)
    grad_proj_bias = jnp.sum(grad_attn, axis=0, dtype=jnp.float32)
    grad_w_proj = jnp.einsum("rc,rd->cd", mixed_rows, grad_attn, preferred_element_type=jnp.float32)
    grad_mixed = jnp.einsum(
        "rd,cd->rc", grad_attn, w_proj, preferred_element_type=jnp.float32
    ).astype(jnp.bfloat16)
    grad_mixed = grad_mixed.reshape(images_here, slot_count, heads_here, HEAD_DIM)
    scores_again = scores_of(queries, key_heads, key_mask, score_scale)
    weights_soft = jnp.exp(scores_again - log_total)
    grad_value = jnp.einsum(
        "bhqk,bqhe->bkhe",
        weights_soft.astype(jnp.bfloat16),
        grad_mixed,
        preferred_element_type=jnp.float32,
    )
    grad_prob = jnp.einsum(
        "bqhe,bkhe->bhqk", grad_mixed, value_heads, preferred_element_type=jnp.float32
    )
    row_dot = jnp.sum(weights_soft * grad_prob, axis=-1, keepdims=True)
    grad_scores = (weights_soft * (grad_prob - row_dot)).astype(jnp.bfloat16)
    grad_query = (
        jnp.einsum("bhqk,bkhe->bqhe", grad_scores, key_heads, preferred_element_type=jnp.float32)
        * score_scale
    )
    grad_key = (
        jnp.einsum("bhqk,bqhe->bkhe", grad_scores, queries, preferred_element_type=jnp.float32)
        * score_scale
    )
    grad_qkv = jnp.stack([grad_query, grad_key, grad_value], axis=2).astype(jnp.bfloat16)
    grad_qkv = grad_qkv.reshape(row_count, 3 * local_width)
    bias_sums = jnp.sum(grad_qkv, axis=0, dtype=jnp.float32).reshape(3, local_width)
    grad_qv_bias = jnp.stack([bias_sums[0], bias_sums[2]])
    grad_w_qkv = jnp.einsum("rd,rc->dc", normed1, grad_qkv, preferred_element_type=jnp.float32)
    grad_w_qkv = grad_w_qkv.reshape(model_width, 3, local_width)
    normed_part = jnp.einsum("rc,dc->rd", grad_qkv, w_flat, preferred_element_type=jnp.float32)
    grad_normed1 = lax.psum(normed_part.astype(jnp.bfloat16), "tensor").astype(jnp.float32)
    grad_norm1_gain = jnp.sum(grad_normed1 * unit1, axis=0)
    grad_norm1_shift = jnp.sum(grad_normed1, axis=0)
    grad_full = grad_middle + norm_back(grad_normed1, unit1, inverse1, norm1_gain)
    grad_input = lax.dynamic_slice_in_dim(grad_full, first_col, col_count, 1) * keep_rows
    input_grad = grad_input.astype(jnp.bfloat16).reshape(images_here, slot_count, col_count)
    summed = (
        lax.psum(grad_norm1_gain.astype(jnp.bfloat16), "dp").astype(jnp.float32),
        lax.psum(grad_norm1_shift.astype(jnp.bfloat16), "dp").astype(jnp.float32),
        lax.psum(grad_w_qkv.astype(jnp.bfloat16), "dp").astype(jnp.float32),
        lax.psum(grad_qv_bias.astype(jnp.bfloat16), "dp").astype(jnp.float32),
        lax.psum(grad_w_proj.astype(jnp.bfloat16), "dp").astype(jnp.float32),
        lax.psum(grad_proj_bias.astype(jnp.bfloat16), "dp").astype(jnp.float32),
        lax.psum(grad_norm2_gain.astype(jnp.bfloat16), "dp").astype(jnp.float32),
        lax.psum(grad_norm2_shift.astype(jnp.bfloat16), "dp").astype(jnp.float32),
        lax.psum(grad_w_fc1.astype(jnp.bfloat16), "dp").astype(jnp.float32),
        lax.psum(grad_fc1_bias.astype(jnp.bfloat16), "dp").astype(jnp.float32),
        lax.psum(grad_w_fc2.astype(jnp.bfloat16), "dp").astype(jnp.float32),
        lax.psum(grad_fc2_bias.astype(jnp.bfloat16), "dp").astype(jnp.float32),
    )
    return (
        output,
        input_grad,
        summed[0],
        summed[1],
        summed[2],
        summed[3],
        summed[4],
        summed[5],
        summed[6],
        summed[7],
        summed[8],
        summed[9],
        summed[10],
        summed[11],
    )


def solution(mesh):
    in_specs = (
        P("dp", None, "tensor"),
        P("dp"),
        P("dp", None, "tensor"),
        P(),
        P(),
        P(None, None, "tensor"),
        P(None, "tensor"),
        P("tensor", None),
        P(),
        P(),
        P(),
        P(None, "tensor"),
        P("tensor"),
        P("tensor", None),
        P(),
    )
    out_specs = (
        P("dp", None, "tensor"),
        P("dp", None, "tensor"),
        P(),
        P(),
        P(None, None, "tensor"),
        P(None, "tensor"),
        P("tensor", None),
        P(),
        P(),
        P(),
        P(None, "tensor"),
        P("tensor"),
        P("tensor", None),
        P(),
    )
    return jax.shard_map(
        per_device, mesh=mesh, in_specs=in_specs, out_specs=out_specs, check_vma=False
    )
```

profile of v0, /device:TPU:0, one launch (start us, length us, event | category | flops | bytes accessed | tf_op | source)
XLA Modules:
  0.0 699.4 jit_solution(9213317824829638723)
XLA Ops:
  12.8 54.3 %all-gather.3.cloned.1.call-done = bf16[4,320,1024]{2,1,0:T(8,128)(2,1)} async-done(((bf16[4,320,256]{2,1,0:T(8,128)(2,1)}), bf16[4,320,1024]{2,1,0:T(8,128)(2,1)}) %all-gather.3.cloned.1.call-update) | async-done | bytes 2621456 | tf_op jit(solution)/shard_map/all_gather | solution.py:64
  75.4 3.5 add_convert_fusion.3
  78.9 6.7 reshape.265
  85.6 4.0 fusion.57
  94.3 3.2 copy.66
  108.7 3.4 convolution_convert_fusion.1
  112.3 9.5 %all-gather.5.cloned.1.call-done = bf16[4,320,1024]{2,1,0:T(8,128)(2,1)} async-done(((bf16[4,320,256]{2,1,0:T(8,128)(2,1)}), bf16[4,320,1024]{2,1,0:T(8,128)(2,1)}) %all-gather.5.cloned.1.call-update) | async-done | bytes 2621456 | tf_op jit(solution)/shard_map/all_gather | solution.py:65
  121.8 105.2 %all-reduce.7.cloned.1.call-done = bf16[1280,1024]{1,0:T(8,128)(2,1)} async-done(((bf16[1280,1024]{1,0:T(8,128)(2,1)}), bf16[1280,1024]{1,0:T(8,128)(2,1)}) %all-reduce.7.cloned.1.call-update) | async-done | bytes 2621456 | tf_op jit(solution)/shard_map/psum | solution.py:96
  227.0 5.0 fusion.56
  238.4 16.8 %fusion.52 = (bf16[1024]{0:T(1024)(128)(2,1)}, bf16[1280,1024]{1,0:T(8,128)(2,1)S(1)}, f32[1280,1024]{1,0:T(8,128)}) fusion(f32[1280,1024]{1,0:T(8,128)S(1)} %fusion.51, f32[1024]{0:T(1024)S(1)} %copy-done.45, bf16[1280,1024]{1,0:T(8,128)(2,1)S(1)} %get-tuple-element.49, bf16[1024,1024]{1,0:T(8,128)(2,1)S(1)} %copy-done), kind=kOutput, calls=%fused_computation.113 | convolution fusion | flops 2781346816 | bytes 17831936 | tf_op jit(solution)/shard_map/rd,fd->rf/dot_general | solution.py:115
  256.6 4.2 convolution_convert_fusion.2
  262.3 101.8 %all-reduce.9.cloned.1.call-done = bf16[1280,1024]{1,0:T(8,128)(2,1)} async-done(((bf16[1280,1024]{1,0:T(8,128)(2,1)}), bf16[1280,1024]{1,0:T(8,128)(2,1)}) %all-reduce.9.cloned.1.call-update) | async-done | bytes 2621456 | tf_op jit(solution)/shard_map/psum | solution.py:121
  364.1 5.5 fusion.9
  369.6 5.6 convert_reduce_fusion
  382.3 3.2 copy.47
  385.5 5.5 fusion.27
  391.1 5.4 multiply_reduce_fusion
  402.2 3.2 copy.52
  405.5 4.7 convert_element_type.226
  410.2 5.7 convolution_convert_fusion
  416.0 5.5 multiply_convert_fusion.2
  423.0 4.1 convolution_convert_fusion.3
  427.4 7.1 %convolution_convert_fusion.5 = bf16[1024,1024]{1,0:T(8,128)(2,1)} fusion(bf16[1280,1024]{1,0:T(8,128)(2,1)} %copy-done.15, bf16[1280,1024]{1,0:T(8,128)(2,1)} %copy-done.12), kind=kOutput, calls=%fused_computation.66 | convolution fusion | flops 2685403136 | bytes 7340032 | tf_op jit(solution)/shard_map/rf,rd->fd/dot_general | solution.py:114
  434.5 7.3 %convolution_convert_fusion.6 = bf16[1024,1024]{1,0:T(8,128)(2,1)} fusion(bf16[1280,1024]{1,0:T(8,128)(2,1)S(1)} %copy-done.52, f32[1280,1024]{1,0:T(8,128)} %copy-done.2, f32[1024]{0:T(1024)S(1)} %copy-done.50, f32[1024]{0:T(1024)S(1)} %copy-done.38, f32[1280]{0:T(1024)S(1)} %copy-done.31, f32[1280]{0:T(1024)S(1)} %copy-done.25), kind=kOutput, calls=%fused_computation.67 | convolution fusion | flops 2691956736 | bytes 9979904 | tf_op jit(solution)/shard_map/rd,rf->df/dot_general | solution.py:119
  444.4 3.4 convolution_convert_fusion.7
  451.3 67.9 %all-reduce.11.cloned.1.call-done = bf16[1280,1024]{1,0:T(8,128)(2,1)} async-done(((bf16[1280,1024]{1,0:T(8,128)(2,1)}), bf16[1280,1024]{1,0:T(8,128)(2,1)}) %all-reduce.11.cloned.1.call-update) | async-done | bytes 2621456 | tf_op jit(solution)/shard_map/psum | solution.py:160
  521.4 7.4 %fusion.10 = (bf16[1024]{0:T(1024)(128)(2,1)S(1)}, f32[1280]{0:T(1024)S(1)}, f32[1280]{0:T(1024)S(1)}, f32[1280,1024]{1,0:T(8,128)}, f32[1280,1024]{1,0:T(8,128)}) fusion(bf16[1280,1024]{1,0:T(8,128)(2,1)} %all-reduce.11.cloned.1.call-done, f32[1280]{0:T(1024)S(1)} %rsqrt.22, f32[1280]{0:T(1024)S(1)} %div.43, f32[1280]{0:T(1024)S(1)} %reshape.262, ...), kind=kLoop, calls=%fused_computation.21 | loop fusion | flops 14414336 | bytes 15760384 | tf_op jit(solution)/shard_map/reduce_sum | solution.py:161
  528.9 24.7 %all-reduce = (bf16[1024]{0:T(1024)(128)(2,1)S(1)}, bf16[1024]{0:T(1024)(128)(2,1)S(1)}, bf16[2,256]{1,0:T(2,128)(2,1)S(1)}, bf16[1024]{0:T(1024)(128)(2,1)S(1)}...) all-reduce(bf16[1024]{0:T(1024)(128)(2,1)S(1)} %get-tuple-element.1, ...), channel_id=1, replica_groups=mesh['dp'=8,'tensor'=4] {'dp'}, use_global_device_ids=true, to_apply=%region_16.17 | all-reduce | flops 7680 | bytes 30720 | tf_op jit(solution)/shard_map/psum | solution.py:167
  558.3 14.9 %reduce-scatter.2.cloned.1.call-done = bf16[1280,256]{1,0:T(8,128)(2,1)} async-done(((bf16[1280,1024]{1,0:T(8,128)(2,1)}), bf16[1280,256]{1,0:T(8,128)(2,1)}) %reduce-scatter.2.cloned.1.call-update) | async-done | bytes 655376 | tf_op jit(solution)/shard_map/reduce_scatter | solution.py:104
  573.2 4.1 fusion.32
  577.3 104.3 %all-reduce.13.cloned.1.call-done = (bf16[1024,3,256]{2,0,1:T(8,128)(2,1)}, bf16[256,1024]{1,0:T(8,128)(2,1)}, bf16[1024,1024]{1,0:T(8,128)(2,1)}, bf16[1024,1024]{1,0:T(8,128)(2,1)}) async-done(((bf16[1024,3,256]{2,0,1:T(8,128)(2,1)}, bf16[256,1024]{1,0:T(8,128)(2,1)}, bf16[1024,1024]{1,0:T(8,128)(2,1)}, bf16[1024,1024]{1,0:T(8,128)(2,1)}), (bf16[1024,3,256]{2,0,1:T(8,128)(2,1)}, ...) | async-done | bytes 6291472 | tf_op jit(solution)/shard_map/psum | solution.py:169
  683.9 3.5 convert_element_type.234
  (183 shorter events, 73.7 us)
Async XLA Ops:
  7.2 231.2 %copy-start = (bf16[1024,1024]{1,0:T(8,128)(2,1)S(1)}, bf16[1024,1024]{1,0:T(8,128)(2,1)}, u32[]{:S(2)}) copy-start(bf16[1024,1024]{1,0:T(8,128)(2,1)} %param.28) | copy-start | bytes 6291460
  7.2 65.4 %copy-start.39 = (f32[1024]{0:T(1024)S(1)}, f32[1024]{0:T(1024)}, u32[]{:S(2)}) copy-start(f32[1024]{0:T(1024)} %param.18) | copy-start | bytes 12292
  7.2 65.3 %copy-start.44 = (f32[1024]{0:T(1024)S(1)}, f32[1024]{0:T(1024)}, u32[]{:S(2)}) copy-start(f32[1024]{0:T(1024)} %param.19) | copy-start | bytes 12292
  7.2 60.0 %all-gather.3.cloned.1.call-start = ((), (), s32[]{:S(2)}) async-start(), calls=%async_computation.1 | async-start | bytes 3276800 | tf_op jit(solution)/shard_map/all_gather | solution.py:64
  8.0 113.8 %all-gather.5.cloned.1.call-start = ((), (), s32[]{:S(2)}) async-start(), calls=%async_computation.4 | async-start | bytes 3276800 | tf_op jit(solution)/shard_map/all_gather | solution.py:65
  8.7 218.3 %all-reduce.7.cloned.1.call-start = ((), (), s32[]{:S(2)}) async-start(), calls=%async_computation.2 | async-start | bytes 5242880 | tf_op jit(solution)/shard_map/psum | solution.py:96
  10.2 92.5 %copy-start.34 = (pred[4,320]{1,0:T(4,128)(4,1)}, pred[4,320]{1,0:T(4,128)(4,1)S(1)}, u32[]{:S(2)}) copy-start(pred[4,320]{1,0:T(4,128)(4,1)S(1)} %get-tuple-element.54) | copy-start | bytes 3844
  67.2 8.2 %copy-start.20 = (bf16[1024,3,256]{0,2,1:T(8,128)(2,1)S(1)}, bf16[1024,3,256]{0,2,1:T(8,128)(2,1)}, u32[]{:S(2)}) copy-start(bf16[1024,3,256]{0,2,1:T(8,128)(2,1)} %copy.39) | copy-start | bytes 4718596
  112.2 251.9 %all-reduce.9.cloned.1.call-start = ((), (), s32[]{:S(2)}) async-start(), calls=%async_computation.5 | async-start | bytes 5242880 | tf_op jit(solution)/shard_map/psum | solution.py:121
  232.0 6.3 copy-start.2
  232.0 6.3 copy-start.12
  232.1 6.2 copy-start.23
  238.3 16.8 %copy-start.8 = (f32[1280,1024]{1,0:T(8,128)}, f32[1280,1024]{1,0:T(8,128)S(1)}, u32[]{:S(2)}) copy-start(f32[1280,1024]{1,0:T(8,128)S(1)} %fusion.51) | copy-start | bytes 15728644
  260.9 258.3 %all-reduce.11.cloned.1.call-start = ((), (), s32[]{:S(2)}) async-start(), calls=%async_computation.6 | async-start | bytes 5242880 | tf_op jit(solution)/shard_map/psum | solution.py:160
  369.6 7.8 %copy-start.18 = (bf16[256,1024]{1,0:T(8,128)(2,1)S(1)}, bf16[256,1024]{1,0:T(8,128)(2,1)}, u32[]{:S(2)}) copy-start(bf16[256,1024]{1,0:T(8,128)(2,1)} %param.22) | copy-start | bytes 1572868
  385.5 11.0 %slice-start = ((s8[7864320]{0:T(1024)(128)(4,1)}), s8[4194304]{0:T(1024)(128)(4,1)S(1)}, s32[]{:S(2)}) async-start(s8[7864320]{0:T(1024)(128)(4,1)} %bitcast.95), calls=%async_computation.8 | async-start | bytes 8388608
  410.2 5.8 copy-start.46
  415.9 157.3 %reduce-scatter.2.cloned.1.call-start = ((), (), s32[]{:S(2)}) async-start(), calls=%async_computation.3 | async-start | bytes 3276800 | tf_op jit(solution)/shard_map/reduce_scatter | solution.py:104
  427.1 7.3 %copy-start.25 = (f32[1280]{0:T(1024)S(1)}, f32[1280]{0:T(1024)}, u32[]{:S(2)}) copy-start(f32[1280]{0:T(1024)} %copy-done.23) | copy-start | bytes 15364
  427.1 7.3 %copy-start.31 = (f32[1280]{0:T(1024)S(1)}, f32[1280]{0:T(1024)}, u32[]{:S(2)}) copy-start(f32[1280]{0:T(1024)} %copy-done.29) | copy-start | bytes 15364
  427.1 7.3 %copy-start.38 = (f32[1024]{0:T(1024)S(1)}, f32[1024]{0:T(1024)}, u32[]{:S(2)}) copy-start(f32[1024]{0:T(1024)} %param.24) | copy-start | bytes 12292
  427.2 7.3 %copy-start.50 = (f32[1024]{0:T(1024)S(1)}, f32[1024]{0:T(1024)}, u32[]{:S(2)}) copy-start(f32[1024]{0:T(1024)} %param.25) | copy-start | bytes 12292
  427.2 254.4 %all-reduce.13.cloned.1.call-start = ((), (), s32[]{:S(2)}) async-start(), calls=%async_computation.7 | async-start | bytes 12582912 | tf_op jit(solution)/shard_map/psum | solution.py:169
  427.4 7.1 %copy-start.52 = (bf16[1280,1024]{1,0:T(8,128)(2,1)S(1)}, bf16[1280,1024]{1,0:T(8,128)(2,1)}, u32[]{:S(2)}) copy-start(bf16[1280,1024]{1,0:T(8,128)(2,1)} %copy-done.51) | copy-start | bytes 7864324
  427.4 14.4 %slice-start.2 = ((s8[5242880]{0:T(1024)(128)(4,1)}), s8[4194304]{0:T(1024)(128)(4,1)S(1)}, s32[]{:S(2)}) async-start(s8[5242880]{0:T(1024)(128)(4,1)} %bitcast.97), calls=%async_computation.10 | async-start | bytes 8388608
  434.5 7.3 %slice-start.3 = ((s8[5242880]{0:T(1024)(128)(4,1)}), s8[1048576]{0:T(1024)(128)(4,1)S(1)}, s32[]{:S(2)}) async-start(s8[5242880]{0:T(1024)(128)(4,1)} %bitcast.97), calls=%async_computation.11 | async-start | bytes 2097152
  447.8 73.6 %copy-start.40 = (f32[1024]{0:T(1024)S(1)}, f32[1024]{0:T(1024)}, u32[]{:S(2)}) copy-start(f32[1024]{0:T(1024)} %param.18) | copy-start | bytes 12292
  521.4 7.5 %copy-start.41 = (bf16[1024]{0:T(1024)(128)(2,1)S(1)}, bf16[1024]{0:T(1024)(128)(2,1)}, u32[]{:S(2)}) copy-start(bf16[1024]{0:T(1024)(128)(2,1)} %get-tuple-element.35) | copy-start | bytes 6148
  521.4 7.5 %copy-start.42 = (bf16[1024]{0:T(1024)(128)(2,1)S(1)}, bf16[1024]{0:T(1024)(128)(2,1)}, u32[]{:S(2)}) copy-start(bf16[1024]{0:T(1024)(128)(2,1)} %get-tuple-element.46) | copy-start | bytes 6148
  521.4 7.5 %copy-start.43 = (bf16[1024]{0:T(1024)(128)(2,1)S(1)}, bf16[1024]{0:T(1024)(128)(2,1)}, u32[]{:S(2)}) copy-start(bf16[1024]{0:T(1024)(128)(2,1)} %get-tuple-element.14) | copy-start | bytes 6148
  521.4 7.5 %copy-start.47 = (bf16[1024]{0:T(1024)(128)(2,1)S(1)}, bf16[1024]{0:T(1024)(128)(2,1)}, u32[]{:S(2)}) copy-start(bf16[1024]{0:T(1024)(128)(2,1)} %get-tuple-element.32) | copy-start | bytes 6148
  683.9 6.0 copy-start.16
  (32 other events, 112.7 us)
Sparse Core Ops, SparseCore 0:
  9.6 57.5 all-gather.2
  68.7 52.9 all-gather.4
  124.7 102.2 all-reduce.6
  261.0 103.0 all-reduce.8
  416.1 103.0 all-reduce.10
  521.9 51.2 reduce-scatter.1
  578.0 103.5 all-reduce.12
where the time goes:
time: 709 us; the launch traced here: 699 us
  waiting for transfers between devices  459 us (65%)
  matrix products  80.7 us (11%)
  other arithmetic  67.8 us (10%)
  local copies, waits for them, and re-layouts  51.3 us (7%)
  blocking collectives  24.7 us (3%)
  between operations  15.1 us (2%)
    psum x1, waiting for transfers between devices, per_device(): lax.psum(attn_part.astype(jnp.bfloat16), 'tensor').astype(jnp.float32)  105 us
    psum x1, waiting for transfers between devices, per_device(): lax.psum(grad_w_qkv.astype(jnp.bfloat16), 'dp').astype(jnp.float32)  104 us
    psum x1, waiting for transfers between devices, per_device(): lax.psum(hidden_part.astype(jnp.bfloat16), 'tensor').astype(jnp.float32)  102 us
    psum x1, waiting for transfers between devices, per_device(): lax.psum(normed_part.astype(jnp.bfloat16), 'tensor').astype(jnp.float32)  67.9 us
    all_gather x1, waiting for transfers between devices, per_device(): lax.all_gather(images, 'tensor', axis=2, tiled=True)  54.3 us
    psum x1, blocking collectives, per_device(): lax.psum(grad_norm1_gain.astype(jnp.bfloat16), 'dp').astype(jnp.float32)  24.7 us
    unnamed x118, local copies, waits for them, and re-layouts  20.9 us
    dot_general x1, matrix products, per_device(): jnp.einsum('rd,fd->rf', grad_ff, w_fc2, preferred_element_type=jnp.float32)  16.8 us
  transfers between devices with their start and end apart: 7, of which 7 were waited for; matrix products, arithmetic and copies ran while one was open for 14% of the time, Pallas kernels for 0%

commit v1 on v0

--- a/solution.py
+++ b/solution.py
@@ -6,6 +6,22 @@
 HEAD_DIM = 64
 EPS = 1e-06
 MASKED = -1e30
+
+
+def ring_gather(x, axis, dim):
+    ways, here, hop = (lax.axis_size(axis), lax.axis_index(axis), x.shape[dim])
+    lengths = [n * ways if d == dim else n for d, n in enumerate(x.shape)]
+    full = lax.dynamic_update_slice_in_dim(jnp.zeros(lengths, x.dtype), x, here * hop, axis=dim)
+    going_up = going_down = x
+    for far in range(1, ways // 2 + 1):
+        going_up = lax.ppermute(going_up, axis, [(d, (d + 1) % ways) for d in range(ways)])
+        full = lax.dynamic_update_slice_in_dim(full, going_up, (here - far) % ways * hop, axis=dim)
+        if 2 * far < ways:
+            going_down = lax.ppermute(going_down, axis, [(d, (d - 1) % ways) for d in range(ways)])
+            full = lax.dynamic_update_slice_in_dim(
+                full, going_down, (here + far) % ways * hop, axis=dim
+            )
+    return full
 
 
 def norm_rows(values, gain_row, shift_row):
@@ -61,7 +77,7 @@
     score_scale = HEAD_DIM ** (-0.5)
     first_col = lax.axis_index("tensor") * col_count
     full_images, full_cot = (
-        lax.all_gather(images, "tensor", axis=2, tiled=True),
+        ring_gather(images, "tensor", 2),
         lax.all_gather(cotangent, "tensor", axis=2, tiled=True),
     )
     slot_ids = jnp.arange(slot_count, dtype=jnp.int32)

time: 709 us -> 725 us (1.023)
  starting transfers between devices: 0.45 us -> 20.2 us
    ppermute x0 -> x3, waiting for transfers between devices: none -> 54.8 us  [the longest x2 36.4 us: ring_gather(): lax.ppermute(going_up, axis, [(d, (d + 1) % ways) for d in range(ways)])]
    all_gather x1 -> x0, waiting for transfers between devices: 54.3 us -> none  [per_device(): lax.all_gather(images, 'tensor', axis=2, tiled=True)]
    ppermute x0 -> x3, starting transfers between devices: none -> 19.8 us  [the longest x2 17.7 us: ring_gather(): lax.ppermute(going_up, axis, [(d, (d + 1) % ways) for d in range(ways)])]
    all_gather x1, waiting for transfers between devices: 9.45 us -> 0.01 us  [per_device(): lax.all_gather(cotangent, 'tensor', axis=2, tiled=True)]
    psum x1, waiting for transfers between devices: 105 us -> 114 us  [per_device(): lax.psum(attn_part.astype(jnp.bfloat16), 'tensor').astype(jnp.float32)]
    unnamed x118 -> x122, local copies, waits for them, and re-layouts: 20.9 us -> 20.9 us
  transfers between devices with their start and end apart: 7 -> 9, of which waited for: 7 -> 8; matrix products, arithmetic and copies ran while one was open for 14% -> 14% of each run, Pallas kernels for 0% -> 0%
where the time goes in v1:
time: 725 us; the launch traced here: 715 us
  waiting for transfers between devices  457 us (63%)
  matrix products  80.7 us (11%)
  other arithmetic  63.6 us (9%)
  local copies, waits for them, and re-layouts  54.1 us (7%)
  blocking collectives  24.7 us (3%)
  starting transfers between devices  20.2 us (3%)
  between operations  15.2 us (2%)
    psum x1, waiting for transfers between devices, per_device(): lax.psum(attn_part.astype(jnp.bfloat16), 'tensor').astype(jnp.float32)  114 us
    psum x1, waiting for transfers between devices, per_device(): lax.psum(grad_w_qkv.astype(jnp.bfloat16), 'dp').astype(jnp.float32)  104 us
    psum x1, waiting for transfers between devices, per_device(): lax.psum(hidden_part.astype(jnp.bfloat16), 'tensor').astype(jnp.float32)  102 us
    psum x1, waiting for transfers between devices, per_device(): lax.psum(normed_part.astype(jnp.bfloat16), 'tensor').astype(jnp.float32)  67.9 us
    ppermute x2, waiting for transfers between devices, ring_gather(): lax.ppermute(going_up, axis, [(d, (d + 1) % ways) for d in range(ways)])  36.4 us
    psum x1, blocking collectives, per_device(): lax.psum(grad_norm1_gain.astype(jnp.bfloat16), 'dp').astype(jnp.float32)  24.7 us
    unnamed x122, local copies, waits for them, and re-layouts  20.9 us
    ppermute x1, waiting for transfers between devices, ring_gather(): lax.ppermute(going_down, axis, [(d, (d - 1) % ways) for d in range(ways)])  18.4 us
  transfers between devices with their start and end apart: 9, of which 8 were waited for; matrix products, arithmetic and copies ran while one was open for 14% of the time, Pallas kernels for 0%

profile of v1, /device:TPU:0, one launch (start us, length us, event | category | flops | bytes accessed | tf_op | source)
XLA Modules:
  0.0 715.5 jit_solution(12717274317932664705)
XLA Ops:
  13.3 18.4 %collective-permute-done = bf16[4,320,256]{2,1,0:T(8,128)(2,1)S(1)} collective-permute-done((bf16[4,320,256]{2,1,0:T(8,128)(2,1)}, bf16[4,320,256]{2,1,0:T(8,128)(2,1)S(1)}, u32[]{:S(2)}, u32[]{:S(2)}) %collective-permute-start) | collective-permute-done | bytes 655392 | tf_op jit(solution)/shard_map/ppermute | solution.py:17
  31.7 14.6 %collective-permute-start.2 = (bf16[4,320,256]{2,1,0:T(8,128)(2,1)S(1)}, bf16[4,320,256]{2,1,0:T(8,128)(2,1)}, u32[]{:S(2)}, u32[]{:S(2)}) collective-permute-start(bf16[4,320,256]{2,1,0:T(8,128)(2,1)S(1)} %collective-permute-done), channel_id=1, source_target_pairs={{0,1},{1,2},{2,3},{3,0},{4,5},{5,6},{6,7},{7,4},{8,9},{9,10},{10,1... | collective-permute-start | bytes 1966088 | tf_op jit(solution)/shard_map/ppermute | solution.py:17
  49.5 18.4 %collective-permute-done.1 = bf16[4,320,256]{2,1,0:T(8,128)(2,1)} collective-permute-done((bf16[4,320,256]{2,1,0:T(8,128)(2,1)}, bf16[4,320,256]{2,1,0:T(8,128)(2,1)}, u32[]{:S(2)}, u32[]{:S(2)}) %collective-permute-start.1) | collective-permute-done | bytes 655392 | tf_op jit(solution)/shard_map/ppermute | solution.py:20
  69.1 18.0 %collective-permute-done.2 = bf16[4,320,256]{2,1,0:T(8,128)(2,1)} collective-permute-done((bf16[4,320,256]{2,1,0:T(8,128)(2,1)S(1)}, bf16[4,320,256]{2,1,0:T(8,128)(2,1)}, u32[]{:S(2)}, u32[]{:S(2)}) %collective-permute-start.2) | collective-permute-done | bytes 655392 | tf_op jit(solution)/shard_map/ppermute | solution.py:17
  92.9 3.5 add_convert_fusion.3
  96.4 6.7 reshape.265
  103.1 3.9 fusion.57
  126.2 3.4 convolution_convert_fusion.1
  129.7 114.1 %all-reduce.7.cloned.1.call-done = bf16[1280,1024]{1,0:T(8,128)(2,1)} async-done(((bf16[1280,1024]{1,0:T(8,128)(2,1)}), bf16[1280,1024]{1,0:T(8,128)(2,1)}) %all-reduce.7.cloned.1.call-update) | async-done | bytes 2621456 | tf_op jit(solution)/shard_map/psum | solution.py:112
  243.8 5.0 fusion.56
  255.2 16.8 %fusion.52 = (bf16[1024]{0:T(1024)(128)(2,1)}, bf16[1280,1024]{1,0:T(8,128)(2,1)S(1)}, f32[1280,1024]{1,0:T(8,128)}) fusion(f32[1280,1024]{1,0:T(8,128)S(1)} %fusion.51, f32[1024]{0:T(1024)S(1)} %copy-done.46, bf16[1280,1024]{1,0:T(8,128)(2,1)S(1)} %get-tuple-element.49, bf16[1024,1024]{1,0:T(8,128)(2,1)S(1)} %copy-done), kind=kOutput, calls=%fused_computation.117 | convolution fusion | flops 2781346816 | bytes 17831936 | tf_op jit(solution)/shard_map/rd,fd->rf/dot_general | solution.py:131
  273.4 4.2 convolution_convert_fusion.2
  279.1 101.8 %all-reduce.9.cloned.1.call-done = bf16[1280,1024]{1,0:T(8,128)(2,1)} async-done(((bf16[1280,1024]{1,0:T(8,128)(2,1)}), bf16[1280,1024]{1,0:T(8,128)(2,1)}) %all-reduce.9.cloned.1.call-update) | async-done | bytes 2621456 | tf_op jit(solution)/shard_map/psum | solution.py:137
  380.9 5.5 fusion.9
  386.4 5.6 convert_reduce_fusion
  402.3 5.5 fusion.27
  407.9 5.4 multiply_reduce_fusion
  419.0 3.2 copy.52
  422.3 4.7 convert_element_type.226
  427.0 5.7 convolution_convert_fusion
  432.8 5.5 multiply_convert_fusion.2
  439.8 4.1 convolution_convert_fusion.3
  444.2 7.0 convolution_convert_fusion.5
  451.3 7.3 %convolution_convert_fusion.6 = bf16[1024,1024]{1,0:T(8,128)(2,1)} fusion(bf16[1280,1024]{1,0:T(8,128)(2,1)S(1)} %copy-done.54, f32[1280,1024]{1,0:T(8,128)} %copy-done.2, f32[1024]{0:T(1024)S(1)} %copy-done.52, f32[1024]{0:T(1024)S(1)} %copy-done.39, f32[1280]{0:T(1024)S(1)} %copy-done.32, f32[1280]{0:T(1024)S(1)} %copy-done.26), kind=kOutput, calls=%fused_computation.67 | convolution fusion | flops 2691956736 | bytes 9979904 | tf_op jit(solution)/shard_map/rd,rf->df/dot_general | solution.py:135
  461.2 3.4 convolution_convert_fusion.7
  468.1 67.9 %all-reduce.11.cloned.1.call-done = bf16[1280,1024]{1,0:T(8,128)(2,1)} async-done(((bf16[1280,1024]{1,0:T(8,128)(2,1)}), bf16[1280,1024]{1,0:T(8,128)(2,1)}) %all-reduce.11.cloned.1.call-update) | async-done | bytes 2621456 | tf_op jit(solution)/shard_map/psum | solution.py:176
  538.3 7.4 %fusion.10 = (bf16[1024]{0:T(1024)(128)(2,1)S(1)}, f32[1280]{0:T(1024)S(1)}, f32[1280]{0:T(1024)S(1)}, f32[1280,1024]{1,0:T(8,128)}, f32[1280,1024]{1,0:T(8,128)}) fusion(bf16[1280,1024]{1,0:T(8,128)(2,1)} %all-reduce.11.cloned.1.call-done, f32[1280]{0:T(1024)S(1)} %rsqrt.22, f32[1280]{0:T(1024)S(1)} %div.43, f32[1280]{0:T(1024)S(1)} %reshape.262, ...), kind=kLoop, calls=%fused_computation.21 | loop fusion | flops 14414336 | bytes 15760384 | tf_op jit(solution)/shard_map/reduce_sum | solution.py:177
  545.7 24.7 %all-reduce = (bf16[1024]{0:T(1024)(128)(2,1)S(1)}, bf16[1024]{0:T(1024)(128)(2,1)S(1)}, bf16[2,256]{1,0:T(2,128)(2,1)S(1)}, bf16[1024]{0:T(1024)(128)(2,1)S(1)}...) all-reduce(bf16[1024]{0:T(1024)(128)(2,1)S(1)} %get-tuple-element.1, ...), channel_id=1, replica_groups=mesh['dp'=8,'tensor'=4] {'dp'}, use_global_device_ids=true, to_apply=%region_16.17 | all-reduce | flops 7680 | bytes 30720 | tf_op jit(solution)/shard_map/psum | solution.py:183
  575.2 14.9 %reduce-scatter.2.cloned.1.call-done = bf16[1280,256]{1,0:T(8,128)(2,1)} async-done(((bf16[1280,1024]{1,0:T(8,128)(2,1)}), bf16[1280,256]{1,0:T(8,128)(2,1)}) %reduce-scatter.2.cloned.1.call-update) | async-done | bytes 655376 | tf_op jit(solution)/shard_map/reduce_scatter | solution.py:120
  590.0 4.1 fusion.32
  594.1 103.6 %all-reduce.13.cloned.1.call-done = (bf16[1024,3,256]{2,0,1:T(8,128)(2,1)}, bf16[256,1024]{1,0:T(8,128)(2,1)}, bf16[1024,1024]{1,0:T(8,128)(2,1)}, bf16[1024,1024]{1,0:T(8,128)(2,1)}) async-done(((bf16[1024,3,256]{2,0,1:T(8,128)(2,1)}, bf16[256,1024]{1,0:T(8,128)(2,1)}, bf16[1024,1024]{1,0:T(8,128)(2,1)}, bf16[1024,1024]{1,0:T(8,128)(2,1)}), (bf16[1024,3,256]{2,0,1:T(8,128)(2,1)}, ...) | async-done | bytes 6291472 | tf_op jit(solution)/shard_map/psum | solution.py:185
  700.0 3.5 convert_element_type.234
  (195 shorter events, 82.5 us)
Async XLA Ops:
  7.2 248.0 %copy-start = (bf16[1024,1024]{1,0:T(8,128)(2,1)S(1)}, bf16[1024,1024]{1,0:T(8,128)(2,1)}, u32[]{:S(2)}) copy-start(bf16[1024,1024]{1,0:T(8,128)(2,1)} %param.28) | copy-start | bytes 6291460
  7.2 42.1 %copy-start.21 = (bf16[4,320,256]{2,1,0:T(8,128)(2,1)S(1)}, bf16[4,320,256]{2,1,0:T(8,128)(2,1)}, u32[]{:S(2)}) copy-start(bf16[4,320,256]{2,1,0:T(8,128)(2,1)} %param.15) | copy-start | bytes 1966084
  7.2 42.2 %copy-start.49 = (s32[4]{0:T(128)S(1)}, s32[4]{0:T(128)}, u32[]{:S(2)}) copy-start(s32[4]{0:T(128)} %param.16) | copy-start | bytes 52
  7.2 122.5 %all-gather.2.cloned.1.call-start = ((), (), s32[]{:S(2)}) async-start(), calls=%async_computation.3 | async-start | bytes 3276800 | tf_op jit(solution)/shard_map/all_gather | solution.py:81
  7.3 24.4 %collective-permute-start = (bf16[4,320,256]{2,1,0:T(8,128)(2,1)}, bf16[4,320,256]{2,1,0:T(8,128)(2,1)S(1)}, u32[]{:S(2)}, u32[]{:S(2)}) collective-permute-start(bf16[4,320,256]{2,1,0:T(8,128)(2,1)} %param.15), channel_id=1, source_target_pairs={{0,1},{1,2},{2,3},{3,0},{4,5},{5,6},{6,7},{7,4},{8,9},{9,10},{10,1... | collective-permute-start | bytes 1966088 | tf_op jit(solution)/shard_map/ppermute | solution.py:17
  10.4 57.5 %collective-permute-start.1 = (bf16[4,320,256]{2,1,0:T(8,128)(2,1)}, bf16[4,320,256]{2,1,0:T(8,128)(2,1)}, u32[]{:S(2)}, u32[]{:S(2)}) collective-permute-start(bf16[4,320,256]{2,1,0:T(8,128)(2,1)} %param.15), channel_id=1, source_target_pairs={{0,3},{1,0},{2,1},{3,2},{4,7},{5,4},{6,5},{7,6},{8,11},{9,8},{10,9... | collective-permute-start | bytes 1966088 | tf_op jit(solution)/shard_map/ppermute | solution.py:20
  12.5 231.3 %all-reduce.7.cloned.1.call-start = ((), (), s32[]{:S(2)}) async-start(), calls=%async_computation.1 | async-start | bytes 5242880 | tf_op jit(solution)/shard_map/psum | solution.py:112
  31.7 55.4 %collective-permute-start.2 = (bf16[4,320,256]{2,1,0:T(8,128)(2,1)S(1)}, bf16[4,320,256]{2,1,0:T(8,128)(2,1)}, u32[]{:S(2)}, u32[]{:S(2)}) collective-permute-start(bf16[4,320,256]{2,1,0:T(8,128)(2,1)S(1)} %collective-permute-done), channel_id=1, source_target_pairs={{0,1},{1,2},{2,3},{3,0},{4,5},{5,6},{6,7},{7,4},{8,9},{9,10},{10,1... | collective-permute-start | bytes 1966088 | tf_op jit(solution)/shard_map/ppermute | solution.py:17
  49.3 40.8 %copy-start.40 = (f32[1024]{0:T(1024)S(1)}, f32[1024]{0:T(1024)}, u32[]{:S(2)}) copy-start(f32[1024]{0:T(1024)} %param.18) | copy-start | bytes 12292
  49.3 40.8 %copy-start.45 = (f32[1024]{0:T(1024)S(1)}, f32[1024]{0:T(1024)}, u32[]{:S(2)}) copy-start(f32[1024]{0:T(1024)} %param.19) | copy-start | bytes 12292
  49.5 70.7 %copy-start.35 = (pred[4,320]{1,0:T(4,128)(4,1)}, pred[4,320]{1,0:T(4,128)(4,1)S(1)}, u32[]{:S(2)}) copy-start(pred[4,320]{1,0:T(4,128)(4,1)S(1)} %get-tuple-element.54) | copy-start | bytes 3844
  129.6 251.3 %all-reduce.9.cloned.1.call-start = ((), (), s32[]{:S(2)}) async-start(), calls=%async_computation.4 | async-start | bytes 5242880 | tf_op jit(solution)/shard_map/psum | solution.py:137
  248.8 6.3 copy-start.2
  248.8 6.3 copy-start.12
  255.1 16.8 %copy-start.8 = (f32[1280,1024]{1,0:T(8,128)}, f32[1280,1024]{1,0:T(8,128)S(1)}, u32[]{:S(2)}) copy-start(f32[1280,1024]{1,0:T(8,128)S(1)} %fusion.51) | copy-start | bytes 15728644
  277.7 258.4 %all-reduce.11.cloned.1.call-start = ((), (), s32[]{:S(2)}) async-start(), calls=%async_computation.5 | async-start | bytes 5242880 | tf_op jit(solution)/shard_map/psum | solution.py:176
  386.4 7.8 %copy-start.18 = (bf16[256,1024]{1,0:T(8,128)(2,1)S(1)}, bf16[256,1024]{1,0:T(8,128)(2,1)}, u32[]{:S(2)}) copy-start(bf16[256,1024]{1,0:T(8,128)(2,1)} %param.22) | copy-start | bytes 1572868
  402.3 11.0 %slice-start = ((s8[7864320]{0:T(1024)(128)(4,1)}), s8[4194304]{0:T(1024)(128)(4,1)S(1)}, s32[]{:S(2)}) async-start(s8[7864320]{0:T(1024)(128)(4,1)} %bitcast.95), calls=%async_computation.7 | async-start | bytes 8388608
  432.8 157.3 %reduce-scatter.2.cloned.1.call-start = ((), (), s32[]{:S(2)}) async-start(), calls=%async_computation.2 | async-start | bytes 3276800 | tf_op jit(solution)/shard_map/reduce_scatter | solution.py:120
  443.9 7.3 %copy-start.26 = (f32[1280]{0:T(1024)S(1)}, f32[1280]{0:T(1024)}, u32[]{:S(2)}) copy-start(f32[1280]{0:T(1024)} %copy-done.24) | copy-start | bytes 15364
  443.9 7.3 %copy-start.32 = (f32[1280]{0:T(1024)S(1)}, f32[1280]{0:T(1024)}, u32[]{:S(2)}) copy-start(f32[1280]{0:T(1024)} %copy-done.30) | copy-start | bytes 15364
  444.0 7.3 %copy-start.39 = (f32[1024]{0:T(1024)S(1)}, f32[1024]{0:T(1024)}, u32[]{:S(2)}) copy-start(f32[1024]{0:T(1024)} %param.24) | copy-start | bytes 12292
  444.0 7.3 %copy-start.52 = (f32[1024]{0:T(1024)S(1)}, f32[1024]{0:T(1024)}, u32[]{:S(2)}) copy-start(f32[1024]{0:T(1024)} %param.25) | copy-start | bytes 12292
  444.0 253.7 %all-reduce.13.cloned.1.call-start = ((), (), s32[]{:S(2)}) async-start(), calls=%async_computation.6 | async-start | bytes 12582912 | tf_op jit(solution)/shard_map/psum | solution.py:185
  444.2 7.1 copy-start.54
  444.2 14.4 %slice-start.2 = ((s8[5242880]{0:T(1024)(128)(4,1)}), s8[4194304]{0:T(1024)(128)(4,1)S(1)}, s32[]{:S(2)}) async-start(s8[5242880]{0:T(1024)(128)(4,1)} %bitcast.97), calls=%async_computation.9 | async-start | bytes 8388608
  451.3 7.3 %slice-start.3 = ((s8[5242880]{0:T(1024)(128)(4,1)}), s8[1048576]{0:T(1024)(128)(4,1)S(1)}, s32[]{:S(2)}) async-start(s8[5242880]{0:T(1024)(128)(4,1)} %bitcast.97), calls=%async_computation.10 | async-start | bytes 2097152
  464.6 73.6 %copy-start.41 = (f32[1024]{0:T(1024)S(1)}, f32[1024]{0:T(1024)}, u32[]{:S(2)}) copy-start(f32[1024]{0:T(1024)} %param.18) | copy-start | bytes 12292
  538.2 7.5 %copy-start.42 = (bf16[1024]{0:T(1024)(128)(2,1)S(1)}, bf16[1024]{0:T(1024)(128)(2,1)}, u32[]{:S(2)}) copy-start(bf16[1024]{0:T(1024)(128)(2,1)} %get-tuple-element.35) | copy-start | bytes 6148
  538.2 7.5 %copy-start.43 = (bf16[1024]{0:T(1024)(128)(2,1)S(1)}, bf16[1024]{0:T(1024)(128)(2,1)}, u32[]{:S(2)}) copy-start(bf16[1024]{0:T(1024)(128)(2,1)} %get-tuple-element.46) | copy-start | bytes 6148
  538.2 7.5 %copy-start.44 = (bf16[1024]{0:T(1024)(128)(2,1)S(1)}, bf16[1024]{0:T(1024)(128)(2,1)}, u32[]{:S(2)}) copy-start(bf16[1024]{0:T(1024)(128)(2,1)} %get-tuple-element.14) | copy-start | bytes 6148
  538.3 7.5 %copy-start.48 = (bf16[1024]{0:T(1024)(128)(2,1)S(1)}, bf16[1024]{0:T(1024)(128)(2,1)}, u32[]{:S(2)}) copy-start(bf16[1024]{0:T(1024)(128)(2,1)} %get-tuple-element.32) | copy-start | bytes 6148
  (36 other events, 131.3 us)
Sparse Core Ops, SparseCore 0:
  12.6 85.1 all-gather.1
  129.7 114.0 all-reduce.6
  277.8 103.0 all-reduce.8
  432.9 103.0 all-reduce.10
  538.7 51.2 reduce-scatter.1
  594.1 103.5 all-reduce.12
